TPU v7x, 32 devices: a whole 2x2x4 slice. The times are simulated.
32 devices in a mesh: dom: 16 (over z, y, x), col: 2 (over core).
Axes of the slice: x: 2, y: 2, z: 4, core: 2. Of those that a mesh axis runs over, the one named last changes fastest.
Arguments:
- features: bfloat16 [16384, 256], P(('dom', 'col')), may hold values from -6 to 6
- weight: bfloat16 [256, 256], replicated, may hold values from -0.375 to 0.375
- cotangent: bfloat16 [16384, 256], P(('dom', 'col')), may hold values from -6 to 6
- tile_values: bfloat16 [1280, 128, 128], P(('dom', 'col')), may hold values from -0.15625 to 0.15625
- tile_rows: int32 [1280], P(('dom', 'col')), may hold values from 0 to 7
- tile_cols: int32 [1280], P(('dom', 'col')), may hold values from 0 to 19, as said below
- tile_count: int32 [32], P(('dom', 'col')), may hold values from 20 to 40, as said below
- send_blocks: int32 [32, 16], P(('dom', 'col')), may hold values from 0 to 3
Outputs:
- output_rows: bfloat16 [16384, 256], P(('dom', 'col'))
- feature_grad: bfloat16 [16384, 256], P(('dom', 'col'))
- weight_grad: float32 [256, 256], replicated
Inputs may be any that keep to these rules, and one draw needn't show every extreme that they name: `tile_cols`: A value v below 4 names the device's own row block v; a value 4 + s names the row block that the device of partition s with the same col index sends to this partition; no receive slot is named by two tiles of one device. Only the first tile_count slots of a device's tiles are live; some device has all 40 live.
All inputs are finite; a program needn't handle non-finite values.
Results may differ from a plain program's by a relative error of at most 0.0049.
Values may be sent and summed in bfloat16 or wider, within the bound.
A program may use at most 128 MiB of HBM per device.

v0:
```python
import jax
import jax.numpy as jnp
from jax import lax
from jax.sharding import PartitionSpec as P


def local(features, weight, cotangent, tile_values, tile_rows, tile_cols, tile_count, send_blocks):
    block_size = tile_values.shape[1]
    half_blocks = features.shape[0] // block_size
    width_in = features.shape[1]
    peer_count = send_blocks.shape[1]
    all_blocks = half_blocks * lax.axis_size("col")
    node_total = features.shape[0] * lax.axis_size("col") * lax.axis_size("dom")
    own_blocks = features.reshape(half_blocks, block_size, width_in)
    outgoing = own_blocks[send_blocks[0]]
    incoming = lax.all_to_all(outgoing, "dom", split_axis=0, concat_axis=0, tiled=True)
    sources = jnp.concatenate([own_blocks, incoming], axis=0)
    live_bool = jnp.arange(tile_values.shape[0], dtype=jnp.int32) < tile_count[0]
    live_mask = live_bool.astype(jnp.bfloat16)
    masked_tiles = tile_values * live_mask[:, None, None]
    picked = sources[tile_cols]
    products = jnp.einsum("tij,tjf->tif", masked_tiles, picked, preferred_element_type=jnp.float32)
    partial_value = jax.ops.segment_sum(products, tile_rows, num_segments=all_blocks)
    summed = lax.psum_scatter(partial_value, "col", scatter_dimension=0, tiled=True)
    hidden = summed.astype(jnp.bfloat16).reshape(half_blocks * block_size, width_in)
    output_rows = jnp.dot(hidden, weight, preferred_element_type=jnp.float32).astype(jnp.bfloat16)
    own_grad = lax.dot_general(
        cotangent, weight, (((1,), (1,)), ((), ())), preferred_element_type=jnp.float32
    ).astype(jnp.bfloat16)
    own_grad = own_grad.reshape(half_blocks, block_size, width_in)
    grad_blocks = lax.all_gather(own_grad, "col", axis=0, tiled=True)
    chosen = grad_blocks[tile_rows]
    back_terms = jnp.einsum(
        "tji,tjf->tif", masked_tiles, chosen, preferred_element_type=jnp.float32
    )
    spread = jax.ops.segment_sum(back_terms, tile_cols, num_segments=half_blocks + peer_count)
    returned = lax.all_to_all(spread[half_blocks:], "dom", split_axis=0, concat_axis=0, tiled=True)
    grad_total = spread[:half_blocks] + jax.ops.segment_sum(
        returned, send_blocks[0], num_segments=half_blocks
    )
    feature_grad = grad_total.astype(jnp.bfloat16).reshape(half_blocks * block_size, width_in)
    local_weight = lax.dot_general(
        hidden, cotangent, (((0,), (0,)), ((), ())), preferred_element_type=jnp.float32
    )
    local_weight = local_weight * jnp.float32(1.0 / node_total**0.5)
    col_share = lax.psum_scatter(local_weight, "col", scatter_dimension=0, tiled=True)
    dom_share = lax.psum(col_share, "dom")
    weight_grad = lax.all_gather(dom_share, "col", axis=0, tiled=True)
    return (output_rows, feature_grad, weight_grad)


def solution(mesh):
    return jax.shard_map(
        local,
        mesh=mesh,
        in_specs=(
            P(("dom", "col"), None),
            P(),
            P(("dom", "col"), None),
            P(("dom", "col"), None, None),
            P(("dom", "col")),
            P(("dom", "col")),
            P(("dom", "col")),
            P(("dom", "col"), None),
        ),
        out_specs=(P(("dom", "col"), None), P(("dom", "col"), None), P()),
        check_vma=False,
    )
```

profile of v0, /device:TPU:0, one launch (start us, length us, event | category | flops | bytes accessed | tf_op | source)
XLA Modules:
  0.0 214.5 jit_solution(6143368337666922137)
XLA Ops:
  7.2 0.0 copy-start
  7.2 0.0 copy-start.7
  7.2 0.0 copy-start.5
  7.2 0.7 fusion.6
  7.9 2.6 %gather_fusion = bf16[16,128,256]{2,1,0:T(8,128)(2,1)} fusion(bf16[4,128,256]{2,1,0:T(8,128)(2,1)} %bitcast.19, s32[1024]{0:T(1024)S(1)} %pad_clamp_fusion.2), kind=kCustom, calls=%fused_computation | custom fusion | bytes 2097216 | tf_op jit(solution)/shard_map/gather | solution.py:15
  10.5 8.4 %all-to-all-start = ((bf16[16,128,256]{2,1,0:T(8,128)(2,1)}), bf16[16,128,256]{2,1,0:T(8,128)(2,1)}, u32[]{:S(2)}, u32[]{:S(2)}) async-start(bf16[16,128,256]{2,1,0:T(8,128)(2,1)} %gather_fusion), calls=%async_computation | async-start | bytes 2097152 | tf_op jit(solution)/shard_map/all_to_all | solution.py:16
  19.5 0.0 copy-done.7
  19.6 0.0 copy-done
  19.6 0.0 copy-done.5
  19.6 0.3 convolution_convert_fusion
  19.9 2.2 %all_gather.6 = bf16[8,128,256]{2,1,0:T(8,128)(2,1)S(1)} all-gather(bf16[4,128,256]{2,1,0:T(8,128)(2,1)S(1)} %bitcast.23), channel_id=1, replica_groups=mesh['dom'=16,'col'=2] {'col'}, dimensions={0}, use_global_device_ids=true | all-gather | bytes 786432 | tf_op jit(solution)/shard_map/all_gather | solution.py:31
  22.0 0.7 gather_fusion.2
  22.8 4.9 %fusion = f32[40,128,256]{2,1,0:T(8,128)} fusion(bf16[40,128,256]{2,1,0:T(8,128)(2,1)S(1)} %gather_fusion.2, bf16[40,128,128]{2,1,0:T(8,128)(2,1)} %param.11, bf16[40]{0:T(256)(128)(2,1)S(1)} %compare_convert_fusion), kind=kOutput, calls=%fused_computation.10 | convolution fusion | flops 336199680 | bytes 9175120 | tf_op jit(solution)/shard_map/tji,tjf->tif/dot_general | solution.py:33
  27.7 0.0 copy-start.6
  27.7 0.3 broadcast_in_dim.24
  28.0 0.4 copy-done.6
  28.4 9.1 %scatter_fusion.1 = f32[20,128,256]{2,1,0:T(8,128)S(1)} fusion(f32[20,128,256]{2,1,0:T(8,128)S(1)} %broadcast_in_dim.24, s32[40]{0:T(128)S(1)} %copy-done.6, f32[40,128,256]{2,1,0:T(8,128)} %fusion), kind=kCustom, calls=%fused_computation.4 | custom fusion | flops 1310720 | bytes 15728800 | tf_op jit(solution)/shard_map/scatter-add | solution.py:36
  37.4 0.0 copy-start.2
  37.4 1.8 slice.15
  39.2 0.0 copy-start.3
  39.2 4.1 %all-to-all-done = bf16[16,128,256]{2,1,0:T(8,128)(2,1)} async-done(((bf16[16,128,256]{2,1,0:T(8,128)(2,1)}), bf16[16,128,256]{2,1,0:T(8,128)(2,1)}, u32[]{:S(2)}, u32[]{:S(2)}) %all-to-all-start) | async-done | bytes 1048608 | tf_op jit(solution)/shard_map/all_to_all | solution.py:16
  43.3 0.0 copy-done.2
  43.3 5.9 %all-to-all-start.1 = ((f32[16,128,256]{2,1,0:T(8,128)}), f32[16,128,256]{2,1,0:T(8,128)}, u32[]{:S(2)}, u32[]{:S(2)}) async-start(f32[16,128,256]{2,1,0:T(8,128)} %slice.15), calls=%async_computation.2 | async-start | bytes 4194304 | tf_op jit(solution)/shard_map/all_to_all | solution.py:37
  49.3 0.0 reduce-scatter.3.cloned.1.call-start
  49.3 0.0 copy-done.3
  49.4 1.3 pad_maximum_fusion
  50.7 0.0 copy-start.4
  50.7 2.4 %gather_fusion.1 = bf16[40,128,256]{2,1,0:T(8,128)(2,1)} fusion(bf16[20,128,256]{2,1,0:T(8,128)(2,1)S(1)} %pad_maximum_fusion, s32[1024]{0:T(1024)S(1)} %pad_clamp_fusion.1), kind=kCustom, calls=%fused_computation.1 | custom fusion | bytes 5243040 | tf_op jit(solution)/shard_map/gather | solution.py:21
  53.1 0.0 copy-done.4
  53.1 4.9 %fusion.2 = f32[40,128,256]{2,1,0:T(8,128)} fusion(bf16[40,128,256]{2,1,0:T(8,128)(2,1)} %gather_fusion.1, bf16[40,128,128]{2,1,0:T(8,128)(2,1)S(1)} %copy-done.4, bf16[40]{0:T(256)(128)(2,1)S(1)} %compare_convert_fusion), kind=kOutput, calls=%fused_computation.12 | convolution fusion | flops 336199680 | bytes 9175120 | tf_op jit(solution)/shard_map/tij,tjf->tif/dot_general | solution.py:22
  58.1 0.1 broadcast_in_dim.21
  58.1 9.0 %scatter_fusion = f32[8,128,256]{2,1,0:T(8,128)S(1)} fusion(f32[8,128,256]{2,1,0:T(8,128)S(1)} %broadcast_in_dim.21, s32[40]{0:T(128)S(1)} %copy-done.7, f32[40,128,256]{2,1,0:T(8,128)} %fusion.2), kind=kCustom, calls=%fused_computation.3 | custom fusion | flops 1310720 | bytes 15728800 | tf_op jit(solution)/shard_map/scatter-add | solution.py:23
  67.2 0.0 copy-start.1
  67.2 0.0 copy-start.8
  67.2 1.1 copy-done.1
  68.3 0.0 reduce-scatter.3.cloned.1.call-update
  68.3 0.0 reduce-scatter.5.cloned.1.call-start
  68.4 9.7 %reduce-scatter.3.cloned.1.call-done = f32[4,128,256]{2,1,0:T(8,128)} async-done(((f32[8,128,256]{2,1,0:T(8,128)}), f32[4,128,256]{2,1,0:T(8,128)}) %reduce-scatter.3.cloned.1.call-update) | async-done | bytes 524304 | tf_op jit(solution)/shard_map/reduce_scatter | solution.py:24
  78.1 1.1 convert_element_type.20
  79.1 1.0 convolution_multiply_fusion
  80.1 0.0 reduce-scatter.5.cloned.1.call-update
  80.1 0.0 all-reduce.2.cloned.1.call-start
  80.2 1.1 slice.14
  81.3 10.0 %all-to-all-done.1 = f32[16,128,256]{2,1,0:T(8,128)} async-done(((f32[16,128,256]{2,1,0:T(8,128)}), f32[16,128,256]{2,1,0:T(8,128)}, u32[]{:S(2)}, u32[]{:S(2)}) %all-to-all-start.1) | async-done | bytes 2097184 | tf_op jit(solution)/shard_map/all_to_all | solution.py:37
  91.2 0.0 copy-done.8
  91.2 3.5 %scatter_fusion.2 = f32[4,128,256]{2,1,0:T(8,128)S(1)} fusion(f32[4,128,256]{2,1,0:T(8,128)S(1)} %slice.14, s32[16]{0:T(128)S(1)} %bitcast.25, f32[16,128,256]{2,1,0:T(8,128)} %all-to-all-done.1), kind=kCustom, calls=%fused_computation.5 | custom fusion | flops 524288 | bytes 6291520 | tf_op jit(solution)/shard_map/scatter-add | solution.py:38
  94.7 0.7 convert_element_type.23
  95.4 0.0 reduce-scatter.5.cloned.1.call-done
  95.4 0.0 all-reduce.2.cloned.1.call-update
  95.5 0.9 convolution_convert_fusion.1
  96.4 108.7 %all-reduce.2.cloned.1.call-done = f32[128,256]{1,0:T(8,128)} async-done(((f32[128,256]{1,0:T(8,128)}), f32[128,256]{1,0:T(8,128)}) %all-reduce.2.cloned.1.call-update) | async-done | bytes 131088 | tf_op jit(solution)/shard_map/psum | solution.py:47
  205.1 2.2 %all_gather.7 = f32[256,256]{1,0:T(8,128)S(1)} all-gather(f32[128,256]{1,0:T(8,128)} %all-reduce.2.cloned.1.call-done), channel_id=1, replica_groups=mesh['dom'=16,'col'=2] {'col'}, dimensions={0}, use_global_device_ids=true | all-gather | bytes 393216 | tf_op jit(solution)/shard_map/all_gather | solution.py:48
  207.3 0.7 copy.20
  (6 shorter events, 0.0 us)
Async XLA Ops:
  7.2 12.4 %copy-start = (bf16[512,256]{1,0:T(8,128)(2,1)S(1)}, bf16[512,256]{1,0:T(8,128)(2,1)}, u32[]{:S(2)}) copy-start(bf16[512,256]{1,0:T(8,128)(2,1)} %param.10) | copy-start | bytes 786436
  7.2 12.4 %copy-start.7 = (s32[40]{0:T(128)S(1)}, s32[40]{0:T(128)}, u32[]{:S(2)}) copy-start(s32[40]{0:T(128)} %param.12) | copy-start | bytes 484
  7.2 12.4 %copy-start.5 = (bf16[256,256]{1,0:T(8,128)(2,1)S(1)}, bf16[256,256]{1,0:T(8,128)(2,1)}, u32[]{:S(2)}) copy-start(bf16[256,256]{1,0:T(8,128)(2,1)} %param.9) | copy-start | bytes 393220
  10.5 32.8 %all-to-all-start = ((bf16[16,128,256]{2,1,0:T(8,128)(2,1)}), bf16[16,128,256]{2,1,0:T(8,128)(2,1)}, u32[]{:S(2)}, u32[]{:S(2)}) async-start(bf16[16,128,256]{2,1,0:T(8,128)(2,1)} %gather_fusion), calls=%async_computation | async-start | bytes 2097152 | tf_op jit(solution)/shard_map/all_to_all | solution.py:16
  27.7 0.7 copy-start.6
  37.4 5.9 %copy-start.2 = (f32[20,128,256]{2,1,0:T(8,128)}, f32[20,128,256]{2,1,0:T(8,128)S(1)}, u32[]{:S(2)}) copy-start(f32[20,128,256]{2,1,0:T(8,128)S(1)} %scatter_fusion.1) | copy-start | bytes 7864324
  39.2 10.1 %copy-start.3 = (bf16[512,256]{1,0:T(8,128)(2,1)S(1)}, bf16[512,256]{1,0:T(8,128)(2,1)}, u32[]{:S(2)}) copy-start(bf16[512,256]{1,0:T(8,128)(2,1)} %param.8) | copy-start | bytes 786436
  43.3 47.9 %all-to-all-start.1 = ((f32[16,128,256]{2,1,0:T(8,128)}), f32[16,128,256]{2,1,0:T(8,128)}, u32[]{:S(2)}, u32[]{:S(2)}) async-start(f32[16,128,256]{2,1,0:T(8,128)} %slice.15), calls=%async_computation.2 | async-start | bytes 4194304 | tf_op jit(solution)/shard_map/all_to_all | solution.py:37
  49.3 28.8 %reduce-scatter.3.cloned.1.call-start = ((), (), s32[]{:S(2)}) async-start(), calls=%async_computation.4 | async-start | bytes 1572864 | tf_op jit(solution)/shard_map/reduce_scatter | solution.py:24
  50.7 2.4 %copy-start.4 = (bf16[40,128,128]{2,1,0:T(8,128)(2,1)S(1)}, bf16[40,128,128]{2,1,0:T(8,128)(2,1)}, u32[]{:S(2)}) copy-start(bf16[40,128,128]{2,1,0:T(8,128)(2,1)} %param.11) | copy-start | bytes 3932164
  67.2 1.1 copy-start.1
  67.2 24.0 %copy-start.8 = (s32[1,16]{1,0:T(1,128)S(1)}, s32[1,16]{1,0:T(1,128)}, u32[]{:S(2)}) copy-start(s32[1,16]{1,0:T(1,128)} %param.15) | copy-start | bytes 196
  68.3 27.1 %reduce-scatter.5.cloned.1.call-start = ((), (), s32[]{:S(2)}) async-start(), calls=%async_computation.5 | async-start | bytes 393216 | tf_op jit(solution)/shard_map/reduce_scatter | solution.py:46
  80.1 125.0 %all-reduce.2.cloned.1.call-start = ((), (), s32[]{:S(2)}) async-start(), calls=%async_computation.6 | async-start | bytes 262144 | tf_op jit(solution)/shard_map/psum | solution.py:47
Sparse Core Ops, SparseCore 0:
  68.4 9.5 reduce-scatter.2
  80.9 8.9 reduce-scatter.4
  95.6 109.4 all-reduce.1
where the time goes:
time: 215 us
  waiting for transfers between devices  133 us (62%)
  other arithmetic  25.5 us (12%)
  between operations  14.6 us (7%)
  starting transfers between devices  14.4 us (7%)
  matrix products  12 us (6%)
  local copies, waits for them, and re-layouts  11.1 us (5%)
  blocking collectives  4.37 us (2%)
    psum x1, waiting for transfers between devices, local(): dom_share = lax.psum(col_share, 'dom')  109 us
    all_to_all x1, waiting for transfers between devices, local(): lax.all_to_all(spread[half_blocks:], 'dom', split_axis=0, concat_axis=0,...  9.95 us
    reduce_scatter x1, waiting for transfers between devices, local(): lax.psum_scatter(partial_value, 'col', scatter_dimension=0, tiled=True)  9.71 us
    scatter-add x1, other arithmetic, local(): jax.ops.segment_sum(back_terms, tile_cols, num_segments=half_blocks + pee...  9.08 us
    scatter-add x1, other arithmetic, local(): jax.ops.segment_sum(products, tile_rows, num_segments=all_blocks)  9.04 us
    all_to_all x1, starting transfers between devices, local(): lax.all_to_all(outgoing, 'dom', split_axis=0, concat_axis=0, tiled=True)  8.39 us
    all_to_all x1, starting transfers between devices, local(): lax.all_to_all(spread[half_blocks:], 'dom', split_axis=0, concat_axis=0,...  5.93 us
    dot_general x1, matrix products, local(): jnp.einsum('tij,tjf->tif', masked_tiles, picked, preferred_element_type=j...  4.93 us
  transfers between devices with their start and end apart: 5, of which 4 were waited for; matrix products, arithmetic and copies ran while one was open for 20% of the time, Pallas kernels for 0%

commit v1 on v0

--- a/solution.py
+++ b/solution.py
@@ -2,6 +2,29 @@
 import jax.numpy as jnp
 from jax import lax
 from jax.sharding import PartitionSpec as P
+
+
+def cut_along(value, dim, size):
+    lengths = value.shape
+    tiles = value.reshape(*lengths[:dim], size, lengths[dim] // size, *lengths[dim + 1 :])
+    return jnp.moveaxis(tiles, dim, 0)
+
+
+def laid_out(blocks, dim):
+    blocks = jnp.moveaxis(blocks, 0, dim)
+    shape = blocks.shape
+    return blocks.reshape(*shape[:dim], shape[dim] * shape[dim + 1], *shape[dim + 2 :])
+
+
+def exchange_in_pairs(x, axis, split_dim, concat_dim):
+    length, position = (lax.axis_size(axis), lax.axis_index(axis))
+    blocks = cut_along(x, split_dim, length)
+    outs = [blocks[position]]
+    for step in range(1, length):
+        sent = blocks[position ^ step]
+        outs.append(lax.ppermute(sent, axis, [(i, i ^ step) for i in range(length)]))
+    blocks = jnp.stack(outs)[position ^ jnp.arange(length)]
+    return laid_out(blocks, concat_dim)
 
 
 def local(features, weight, cotangent, tile_values, tile_rows, tile_cols, tile_count, send_blocks):
@@ -34,7 +57,7 @@
         "tji,tjf->tif", masked_tiles, chosen, preferred_element_type=jnp.float32
     )
     spread = jax.ops.segment_sum(back_terms, tile_cols, num_segments=half_blocks + peer_count)
-    returned = lax.all_to_all(spread[half_blocks:], "dom", split_axis=0, concat_axis=0, tiled=True)
+    returned = exchange_in_pairs(spread[half_blocks:], "dom", 0, 0)
     grad_total = spread[:half_blocks] + jax.ops.segment_sum(
         returned, send_blocks[0], num_segments=half_blocks
     )

time: 215 us -> 247 us (1.15)
  starting transfers between devices: 14.4 us -> 43.2 us
  local copies, waits for them, and re-layouts: 11.1 us -> 32.7 us
  waiting for transfers between devices: 133 us -> 115 us
    ppermute x0 -> x15, starting transfers between devices: none -> 34.5 us  [exchange_in_pairs(): lax.ppermute(sent, axis, [(i, i ^ step) for i in range(length)])]
    unnamed x19 -> x46, local copies, waits for them, and re-layouts: 2.2 us -> 19.3 us
    all_to_all x1 -> x0, waiting for transfers between devices: 9.95 us -> none  [local(): lax.all_to_all(spread[half_blocks:], 'dom', split_axis=0, concat_axis=0,...]
    reduce_scatter x1, waiting for transfers between devices: 9.71 us -> 0.01 us  [local(): lax.psum_scatter(partial_value, 'col', scatter_dimension=0, tiled=True)]
    all_to_all x1 -> x0, starting transfers between devices: 5.93 us -> none  [local(): lax.all_to_all(spread[half_blocks:], 'dom', split_axis=0, concat_axis=0,...]
    all_to_all x1, waiting for transfers between devices: 4.13 us -> 0.01 us  [local(): lax.all_to_all(outgoing, 'dom', split_axis=0, concat_axis=0, tiled=True)]
    ppermute x0 -> x15, waiting for transfers between devices: none -> 3.65 us  [exchange_in_pairs(): lax.ppermute(sent, axis, [(i, i ^ step) for i in range(length)])]
    squeeze x0 -> x1, local copies, waits for them, and re-layouts: none -> 2.82 us  [exchange_in_pairs(): sent = blocks[position ^ step]]
  transfers between devices with their start and end apart: 5 -> 19, of which waited for: 4 -> 4; matrix products, arithmetic and copies ran while one was open for 20% -> 26% of each run, Pallas kernels for 0% -> 0%
where the time goes in v1:
time: 247 us
  waiting for transfers between devices  115 us (47%)
  starting transfers between devices  43.2 us (17%)
  local copies, waits for them, and re-layouts  32.7 us (13%)
  other arithmetic  24.2 us (10%)
  between operations  14.7 us (6%)
  matrix products  12.1 us (5%)
  blocking collectives  4.37 us (2%)
    psum x1, waiting for transfers between devices, local(): dom_share = lax.psum(col_share, 'dom')  111 us
    ppermute x15, starting transfers between devices, exchange_in_pairs(): lax.ppermute(sent, axis, [(i, i ^ step) for i in range(length)])  34.5 us
    unnamed x46, local copies, waits for them, and re-layouts  19.3 us
    scatter-add x1, other arithmetic, local(): jax.ops.segment_sum(back_terms, tile_cols, num_segments=half_blocks + pee...  9.08 us
    scatter-add x1, other arithmetic, local(): jax.ops.segment_sum(products, tile_rows, num_segments=all_blocks)  9.04 us
    all_to_all x1, starting transfers between devices, local(): lax.all_to_all(outgoing, 'dom', split_axis=0, concat_axis=0, tiled=True)  8.52 us
    dot_general x1, matrix products, local(): jnp.einsum('tij,tjf->tif', masked_tiles, picked, preferred_element_type=j...  4.99 us
    dot_general x1, matrix products, local(): jnp.einsum('tji,tjf->tif', masked_tiles, chosen, preferred_element_type=j...  4.98 us
  transfers between devices with their start and end apart: 19, of which 4 were waited for; matrix products, arithmetic and copies ran while one was open for 26% of the time, Pallas kernels for 0%

profile of v1, /device:TPU:0, one launch (start us, length us, event | category | flops | bytes accessed | tf_op | source)
XLA Modules:
  0.0 246.6 jit_solution(8119187855748518487)
XLA Ops:
  7.2 0.7 fusion.6
  7.9 2.6 %gather_fusion = bf16[16,128,256]{2,1,0:T(8,128)(2,1)} fusion(bf16[4,128,256]{2,1,0:T(8,128)(2,1)} %bitcast.54, s32[1024]{0:T(1024)S(1)} %pad_clamp_fusion.3), kind=kCustom, calls=%fused_computation | custom fusion | bytes 2097216 | tf_op jit(solution)/shard_map/gather | solution.py:38
  10.5 8.5 %all-to-all-start = ((bf16[16,128,256]{2,1,0:T(8,128)(2,1)}), bf16[16,128,256]{2,1,0:T(8,128)(2,1)}, u32[]{:S(2)}, u32[]{:S(2)}) async-start(bf16[16,128,256]{2,1,0:T(8,128)(2,1)} %gather_fusion), calls=%async_computation | async-start | bytes 2097152 | tf_op jit(solution)/shard_map/all_to_all | solution.py:39
  19.0 0.0 reduce-scatter.3.cloned.1.call-start
  19.8 0.3 convolution_convert_fusion
  20.0 2.2 all_gather.6
  22.2 0.7 gather_fusion.2
  23.0 5.0 %fusion = f32[40,128,256]{2,1,0:T(8,128)} fusion(bf16[40,128,256]{2,1,0:T(8,128)(2,1)S(1)} %gather_fusion.2, bf16[40,128,128]{2,1,0:T(8,128)(2,1)} %param.11, bf16[40]{0:T(256)(128)(2,1)S(1)} %compare_convert_fusion), kind=kOutput, calls=%fused_computation.11 | convolution fusion | flops 336199680 | bytes 9175120 | tf_op jit(solution)/shard_map/tji,tjf->tif/dot_general | solution.py:56
  28.0 0.3 broadcast_in_dim.25
  28.2 0.4 copy-done.12
  28.6 9.1 %scatter_fusion.1 = f32[20,128,256]{2,1,0:T(8,128)S(1)} fusion(f32[20,128,256]{2,1,0:T(8,128)S(1)} %broadcast_in_dim.25, s32[40]{0:T(128)S(1)} %copy-done.12, f32[40,128,256]{2,1,0:T(8,128)} %fusion), kind=kCustom, calls=%fused_computation.5 | custom fusion | flops 1310720 | bytes 15728800 | tf_op jit(solution)/shard_map/scatter-add | solution.py:59
  37.7 1.6 slice.17
  39.3 2.8 %constant_dynamic-slice_fusion = (f32[1,128,256]{2,1,0:T(8,128)}, f32[1,128,256]{2,1,0:T(8,128)}, f32[1,128,256]{2,1,0:T(8,128)}, f32[1,128,256]{2,1,0:T(8,128)}...) fusion(f32[16,128,256]{2,1,0:T(8,128)} %slice.17, ...), kind=kLoop, calls=%fused_computation.37 | loop fusion | bytes 3932220 | tf_op jit(solution)/shard_map/squeeze | solution.py:24
  42.1 1.9 collective-permute-start
  44.0 1.5 collective-permute-start.1
  45.5 0.2 collective-permute-start.2
  45.6 1.9 collective-permute-start.3
  47.5 1.5 collective-permute-start.4
  49.0 1.6 bitcast_dynamic-update-slice_fusion.15
  50.6 2.4 collective-permute-start.5
  53.0 1.6 bitcast_dynamic-update-slice_fusion.14
  54.6 0.2 collective-permute-start.6
  54.8 1.6 bitcast_dynamic-update-slice_fusion.13
  56.4 1.4 pad_maximum_fusion
  57.7 2.4 gather_fusion.1
  60.1 5.0 %fusion.2 = f32[40,128,256]{2,1,0:T(8,128)} fusion(bf16[40,128,256]{2,1,0:T(8,128)(2,1)} %gather_fusion.1, bf16[40,128,128]{2,1,0:T(8,128)(2,1)S(1)} %copy-done.2, bf16[40]{0:T(256)(128)(2,1)S(1)} %compare_convert_fusion), kind=kOutput, calls=%fused_computation.13 | convolution fusion | flops 336199680 | bytes 9175120 | tf_op jit(solution)/shard_map/tij,tjf->tif/dot_general | solution.py:45
  65.1 0.1 broadcast_in_dim.22
  65.2 9.0 %scatter_fusion = f32[8,128,256]{2,1,0:T(8,128)S(1)} fusion(f32[8,128,256]{2,1,0:T(8,128)S(1)} %broadcast_in_dim.22, s32[40]{0:T(128)S(1)} %copy-done.13, f32[40,128,256]{2,1,0:T(8,128)} %fusion.2), kind=kCustom, calls=%fused_computation.4 | custom fusion | flops 1310720 | bytes 15728800 | tf_op jit(solution)/shard_map/scatter-add | solution.py:46
  74.3 0.9 copy-done.1
  75.3 0.0 reduce-scatter.5.cloned.1.call-start
  75.3 2.8 %collective-permute-start.7 = (f32[1,128,256]{2,1,0:T(8,128)S(1)}, f32[1,128,256]{2,1,0:T(8,128)S(1)}, u32[]{:S(2)}, u32[]{:S(2)}) collective-permute-start(f32[1,128,256]{2,1,0:T(8,128)S(1)} %copy-done.11), channel_id=1, source_target_pairs={{0,16},{2,18},{4,20},{6,22},{8,24},{10,26},{12,28},{14,30},{16,0},... | collective-permute-start | bytes 393224 | tf_op jit(solution)/shard_map/ppermute | solution.py:25
  78.2 1.6 bitcast_dynamic-update-slice_fusion.12
  79.7 1.4 collective-permute-start.8
  81.2 1.6 bitcast_dynamic-update-slice_fusion.11
  82.7 3.3 %collective-permute-start.9 = (f32[1,128,256]{2,1,0:T(8,128)S(1)}, f32[1,128,256]{2,1,0:T(8,128)S(1)}, u32[]{:S(2)}, u32[]{:S(2)}) collective-permute-start(f32[1,128,256]{2,1,0:T(8,128)S(1)} %copy-done.9), channel_id=1, source_target_pairs={{0,20},{2,22},{4,16},{6,18},{8,28},{10,30},{12,24},{14,26},{16,4},... | collective-permute-start | bytes 393224 | tf_op jit(solution)/shard_map/ppermute | solution.py:25
  86.0 1.6 bitcast_dynamic-update-slice_fusion.10
  87.6 0.2 collective-permute-start.10
  87.8 1.6 bitcast_dynamic-update-slice_fusion.9
  89.3 3.7 %collective-permute-start.11 = (f32[1,128,256]{2,1,0:T(8,128)S(1)}, f32[1,128,256]{2,1,0:T(8,128)S(1)}, u32[]{:S(2)}, u32[]{:S(2)}) collective-permute-start(f32[1,128,256]{2,1,0:T(8,128)S(1)} %copy-done.7), channel_id=1, source_target_pairs={{0,24},{2,26},{4,28},{6,30},{8,16},{10,18},{12,20},{14,22},{16,8},... | collective-permute-start | bytes 393224 | tf_op jit(solution)/shard_map/ppermute | solution.py:25
  93.0 1.6 bitcast_dynamic-update-slice_fusion.8
  94.6 4.1 %collective-permute-start.12 = (f32[1,128,256]{2,1,0:T(8,128)S(1)}, f32[1,128,256]{2,1,0:T(8,128)S(1)}, u32[]{:S(2)}, u32[]{:S(2)}) collective-permute-start(f32[1,128,256]{2,1,0:T(8,128)S(1)} %copy-done.6), channel_id=1, source_target_pairs={{0,26},{2,24},{4,30},{6,28},{8,18},{10,16},{12,22},{14,20},{16,10}... | collective-permute-start | bytes 393224 | tf_op jit(solution)/shard_map/ppermute | solution.py:25
  98.7 0.7 bitcast_dynamic-update-slice_fusion.7
  99.4 0.6 collective-permute-done.8
  100.0 4.0 %collective-permute-start.13 = (f32[1,128,256]{2,1,0:T(8,128)S(1)}, f32[1,128,256]{2,1,0:T(8,128)S(1)}, u32[]{:S(2)}, u32[]{:S(2)}) collective-permute-start(f32[1,128,256]{2,1,0:T(8,128)S(1)} %copy-done.5), channel_id=1, source_target_pairs={{0,28},{2,30},{4,24},{6,26},{8,20},{10,22},{12,16},{14,18},{16,12}... | collective-permute-start | bytes 393224 | tf_op jit(solution)/shard_map/ppermute | solution.py:25
  104.0 0.7 bitcast_dynamic-update-slice_fusion.6
  104.7 5.6 %collective-permute-start.14 = (f32[1,128,256]{2,1,0:T(8,128)S(1)}, f32[1,128,256]{2,1,0:T(8,128)S(1)}, u32[]{:S(2)}, u32[]{:S(2)}) collective-permute-start(f32[1,128,256]{2,1,0:T(8,128)S(1)} %copy-done.4), channel_id=1, source_target_pairs={{0,30},{2,28},{4,26},{6,24},{8,22},{10,20},{12,18},{14,16},{16,14}... | collective-permute-start | bytes 393224 | tf_op jit(solution)/shard_map/ppermute | solution.py:25
  110.3 0.7 bitcast_dynamic-update-slice_fusion.5
  111.0 3.0 %collective-permute-done.10 = f32[1,128,256]{2,1,0:T(8,128)S(1)} collective-permute-done((f32[1,128,256]{2,1,0:T(8,128)S(1)}, f32[1,128,256]{2,1,0:T(8,128)S(1)}, u32[]{:S(2)}, u32[]{:S(2)}) %collective-permute-start.10) | collective-permute-done | bytes 131104 | tf_op jit(solution)/shard_map/ppermute | solution.py:25
  113.9 0.7 bitcast_dynamic-update-slice_fusion.4
  114.6 0.7 bitcast_dynamic-update-slice_fusion.3
  115.3 1.1 convert_element_type.20
  116.4 1.0 convolution_multiply_fusion
  117.4 0.0 all-reduce.2.cloned.1.call-start
  117.4 0.7 bitcast_dynamic-update-slice_fusion.2
  118.1 0.7 bitcast_dynamic-update-slice_fusion.1
  118.7 0.7 bitcast_dynamic-update-slice_fusion
  119.4 2.3 gather_fusion.3
  121.7 2.2 scatter_fusion.2
  123.9 0.7 convert_element_type.23
  124.6 0.5 reduce-scatter.5.cloned.1.call-done
  125.2 0.9 convolution_convert_fusion.1
  126.1 111.1 %all-reduce.2.cloned.1.call-done = f32[128,256]{1,0:T(8,128)} async-done(((f32[128,256]{1,0:T(8,128)}), f32[128,256]{1,0:T(8,128)}) %all-reduce.2.cloned.1.call-update) | async-done | bytes 131088 | tf_op jit(solution)/shard_map/psum | solution.py:70
  237.2 2.2 all_gather.7
  239.4 0.7 copy.35
  (55 shorter events, 0.2 us)
Async XLA Ops:
  7.2 12.6 %copy-start = (bf16[512,256]{1,0:T(8,128)(2,1)S(1)}, bf16[512,256]{1,0:T(8,128)(2,1)}, u32[]{:S(2)}) copy-start(bf16[512,256]{1,0:T(8,128)(2,1)} %param.10) | copy-start | bytes 786436
  7.9 11.9 %copy-start.3 = (bf16[256,256]{1,0:T(8,128)(2,1)S(1)}, bf16[256,256]{1,0:T(8,128)(2,1)}, u32[]{:S(2)}) copy-start(bf16[256,256]{1,0:T(8,128)(2,1)} %param.9) | copy-start | bytes 393220
  10.5 11.8 %copy-start.13 = (s32[40]{0:T(128)S(1)}, s32[40]{0:T(128)}, u32[]{:S(2)}) copy-start(s32[40]{0:T(128)} %param.12) | copy-start | bytes 484
  10.5 45.9 %all-to-all-start = ((bf16[16,128,256]{2,1,0:T(8,128)(2,1)}), bf16[16,128,256]{2,1,0:T(8,128)(2,1)}, u32[]{:S(2)}, u32[]{:S(2)}) async-start(bf16[16,128,256]{2,1,0:T(8,128)(2,1)} %gather_fusion), calls=%async_computation | async-start | bytes 2097152 | tf_op jit(solution)/shard_map/all_to_all | solution.py:39
  19.0 96.3 %reduce-scatter.3.cloned.1.call-start = ((), (), s32[]{:S(2)}) async-start(), calls=%async_computation.3 | async-start | bytes 1572864 | tf_op jit(solution)/shard_map/reduce_scatter | solution.py:47
  28.0 0.7 copy-start.12
  42.1 8.6 %collective-permute-start = (f32[1,128,256]{2,1,0:T(8,128)}, f32[1,128,256]{2,1,0:T(8,128)}, u32[]{:S(2)}, u32[]{:S(2)}) collective-permute-start(f32[1,128,256]{2,1,0:T(8,128)} %get-tuple-element.17), channel_id=1, source_target_pairs={{0,2},{2,0},{4,6},{6,4},{8,10},{10,8},{12,14},{14,12},{16,18},{18,... | collective-permute-start | bytes 393224 | tf_op jit(solution)/shard_map/ppermute | solution.py:25
  44.0 10.6 %collective-permute-start.1 = (f32[1,128,256]{2,1,0:T(8,128)}, f32[1,128,256]{2,1,0:T(8,128)}, u32[]{:S(2)}, u32[]{:S(2)}) collective-permute-start(f32[1,128,256]{2,1,0:T(8,128)} %get-tuple-element.16), channel_id=1, source_target_pairs={{0,4},{2,6},{4,0},{6,2},{8,12},{10,14},{12,8},{14,10},{16,20},{18,... | collective-permute-start | bytes 393224 | tf_op jit(solution)/shard_map/ppermute | solution.py:25
  45.5 29.9 %collective-permute-start.2 = (f32[1,128,256]{2,1,0:T(8,128)}, f32[1,128,256]{2,1,0:T(8,128)}, u32[]{:S(2)}, u32[]{:S(2)}) collective-permute-start(f32[1,128,256]{2,1,0:T(8,128)} %get-tuple-element.15), channel_id=1, source_target_pairs={{0,6},{2,4},{4,2},{6,0},{8,14},{10,12},{12,10},{14,8},{16,22},{18,... | collective-permute-start | bytes 393224 | tf_op jit(solution)/shard_map/ppermute | solution.py:25
  45.6 34.1 %collective-permute-start.3 = (f32[1,128,256]{2,1,0:T(8,128)}, f32[1,128,256]{2,1,0:T(8,128)}, u32[]{:S(2)}, u32[]{:S(2)}) collective-permute-start(f32[1,128,256]{2,1,0:T(8,128)} %get-tuple-element.14), channel_id=1, source_target_pairs={{0,8},{2,10},{4,12},{6,14},{8,0},{10,2},{12,4},{14,6},{16,24},{18,... | collective-permute-start | bytes 393224 | tf_op jit(solution)/shard_map/ppermute | solution.py:25
  47.5 35.2 %collective-permute-start.4 = (f32[1,128,256]{2,1,0:T(8,128)}, f32[1,128,256]{2,1,0:T(8,128)}, u32[]{:S(2)}, u32[]{:S(2)}) collective-permute-start(f32[1,128,256]{2,1,0:T(8,128)} %get-tuple-element.13), channel_id=1, source_target_pairs={{0,10},{2,8},{4,14},{6,12},{8,2},{10,0},{12,6},{14,4},{16,26},{18,... | collective-permute-start | bytes 393224 | tf_op jit(solution)/shard_map/ppermute | solution.py:25
  50.6 36.9 %collective-permute-start.5 = (f32[1,128,256]{2,1,0:T(8,128)}, f32[1,128,256]{2,1,0:T(8,128)}, u32[]{:S(2)}, u32[]{:S(2)}) collective-permute-start(f32[1,128,256]{2,1,0:T(8,128)} %get-tuple-element.12), channel_id=1, source_target_pairs={{0,12},{2,14},{4,8},{6,10},{8,4},{10,6},{12,0},{14,2},{16,28},{18,... | collective-permute-start | bytes 393224 | tf_op jit(solution)/shard_map/ppermute | solution.py:25
  54.6 34.7 %collective-permute-start.6 = (f32[1,128,256]{2,1,0:T(8,128)}, f32[1,128,256]{2,1,0:T(8,128)}, u32[]{:S(2)}, u32[]{:S(2)}) collective-permute-start(f32[1,128,256]{2,1,0:T(8,128)} %get-tuple-element.11), channel_id=1, source_target_pairs={{0,14},{2,12},{4,10},{6,8},{8,6},{10,4},{12,2},{14,0},{16,30},{18,... | collective-permute-start | bytes 393224 | tf_op jit(solution)/shard_map/ppermute | solution.py:25
  57.7 2.4 copy-start.2
  65.2 10.2 %copy-start.11 = (f32[1,128,256]{2,1,0:T(8,128)S(1)}, f32[1,128,256]{2,1,0:T(8,128)}, u32[]{:S(2)}) copy-start(f32[1,128,256]{2,1,0:T(8,128)} %get-tuple-element.10) | copy-start | bytes 393220
  65.2 14.5 %copy-start.10 = (f32[1,128,256]{2,1,0:T(8,128)S(1)}, f32[1,128,256]{2,1,0:T(8,128)}, u32[]{:S(2)}) copy-start(f32[1,128,256]{2,1,0:T(8,128)} %get-tuple-element.9) | copy-start | bytes 393220
  65.2 17.5 %copy-start.9 = (f32[1,128,256]{2,1,0:T(8,128)S(1)}, f32[1,128,256]{2,1,0:T(8,128)}, u32[]{:S(2)}) copy-start(f32[1,128,256]{2,1,0:T(8,128)} %get-tuple-element.8) | copy-start | bytes 393220
  65.2 22.4 %copy-start.8 = (f32[1,128,256]{2,1,0:T(8,128)S(1)}, f32[1,128,256]{2,1,0:T(8,128)}, u32[]{:S(2)}) copy-start(f32[1,128,256]{2,1,0:T(8,128)} %get-tuple-element.7) | copy-start | bytes 393220
  74.3 1.0 copy-start.1
  74.3 15.1 %copy-start.7 = (f32[1,128,256]{2,1,0:T(8,128)S(1)}, f32[1,128,256]{2,1,0:T(8,128)}, u32[]{:S(2)}) copy-start(f32[1,128,256]{2,1,0:T(8,128)} %get-tuple-element.6) | copy-start | bytes 393220
  74.3 20.3 %copy-start.6 = (f32[1,128,256]{2,1,0:T(8,128)S(1)}, f32[1,128,256]{2,1,0:T(8,128)}, u32[]{:S(2)}) copy-start(f32[1,128,256]{2,1,0:T(8,128)} %get-tuple-element.5) | copy-start | bytes 393220
  74.3 25.7 %copy-start.5 = (f32[1,128,256]{2,1,0:T(8,128)S(1)}, f32[1,128,256]{2,1,0:T(8,128)}, u32[]{:S(2)}) copy-start(f32[1,128,256]{2,1,0:T(8,128)} %get-tuple-element.4) | copy-start | bytes 393220
  74.3 30.4 %copy-start.4 = (f32[1,128,256]{2,1,0:T(8,128)S(1)}, f32[1,128,256]{2,1,0:T(8,128)}, u32[]{:S(2)}) copy-start(f32[1,128,256]{2,1,0:T(8,128)} %get-tuple-element.3) | copy-start | bytes 393220
  75.3 49.9 %reduce-scatter.5.cloned.1.call-start = ((), (), s32[]{:S(2)}) async-start(), calls=%async_computation.4 | async-start | bytes 393216 | tf_op jit(solution)/shard_map/reduce_scatter | solution.py:69
  75.3 19.2 %collective-permute-start.7 = (f32[1,128,256]{2,1,0:T(8,128)S(1)}, f32[1,128,256]{2,1,0:T(8,128)S(1)}, u32[]{:S(2)}, u32[]{:S(2)}) collective-permute-start(f32[1,128,256]{2,1,0:T(8,128)S(1)} %copy-done.11), channel_id=1, source_target_pairs={{0,16},{2,18},{4,20},{6,22},{8,24},{10,26},{12,28},{14,30},{16,0},... | collective-permute-start | bytes 393224 | tf_op jit(solution)/shard_map/ppermute | solution.py:25
  79.7 20.3 %collective-permute-start.8 = (f32[1,128,256]{2,1,0:T(8,128)S(1)}, f32[1,128,256]{2,1,0:T(8,128)S(1)}, u32[]{:S(2)}, u32[]{:S(2)}) collective-permute-start(f32[1,128,256]{2,1,0:T(8,128)S(1)} %copy-done.10), channel_id=1, source_target_pairs={{0,18},{2,16},{4,22},{6,20},{8,26},{10,24},{12,30},{14,28},{16,2},... | collective-permute-start | bytes 393224 | tf_op jit(solution)/shard_map/ppermute | solution.py:25
  82.7 22.0 %collective-permute-start.9 = (f32[1,128,256]{2,1,0:T(8,128)S(1)}, f32[1,128,256]{2,1,0:T(8,128)S(1)}, u32[]{:S(2)}, u32[]{:S(2)}) collective-permute-start(f32[1,128,256]{2,1,0:T(8,128)S(1)} %copy-done.9), channel_id=1, source_target_pairs={{0,20},{2,22},{4,16},{6,18},{8,28},{10,30},{12,24},{14,26},{16,4},... | collective-permute-start | bytes 393224 | tf_op jit(solution)/shard_map/ppermute | solution.py:25
  87.6 26.3 %collective-permute-start.10 = (f32[1,128,256]{2,1,0:T(8,128)S(1)}, f32[1,128,256]{2,1,0:T(8,128)S(1)}, u32[]{:S(2)}, u32[]{:S(2)}) collective-permute-start(f32[1,128,256]{2,1,0:T(8,128)S(1)} %copy-done.8), channel_id=1, source_target_pairs={{0,22},{2,20},{4,18},{6,16},{8,30},{10,28},{12,26},{14,24},{16,6},... | collective-permute-start | bytes 393224 | tf_op jit(solution)/shard_map/ppermute | solution.py:25
  89.3 25.3 %collective-permute-start.11 = (f32[1,128,256]{2,1,0:T(8,128)S(1)}, f32[1,128,256]{2,1,0:T(8,128)S(1)}, u32[]{:S(2)}, u32[]{:S(2)}) collective-permute-start(f32[1,128,256]{2,1,0:T(8,128)S(1)} %copy-done.7), channel_id=1, source_target_pairs={{0,24},{2,26},{4,28},{6,30},{8,16},{10,18},{12,20},{14,22},{16,8},... | collective-permute-start | bytes 393224 | tf_op jit(solution)/shard_map/ppermute | solution.py:25
  94.6 22.8 %collective-permute-start.12 = (f32[1,128,256]{2,1,0:T(8,128)S(1)}, f32[1,128,256]{2,1,0:T(8,128)S(1)}, u32[]{:S(2)}, u32[]{:S(2)}) collective-permute-start(f32[1,128,256]{2,1,0:T(8,128)S(1)} %copy-done.6), channel_id=1, source_target_pairs={{0,26},{2,24},{4,30},{6,28},{8,18},{10,16},{12,22},{14,20},{16,10}... | collective-permute-start | bytes 393224 | tf_op jit(solution)/shard_map/ppermute | solution.py:25
  100.0 18.1 %collective-permute-start.13 = (f32[1,128,256]{2,1,0:T(8,128)S(1)}, f32[1,128,256]{2,1,0:T(8,128)S(1)}, u32[]{:S(2)}, u32[]{:S(2)}) collective-permute-start(f32[1,128,256]{2,1,0:T(8,128)S(1)} %copy-done.5), channel_id=1, source_target_pairs={{0,28},{2,30},{4,24},{6,26},{8,20},{10,22},{12,16},{14,18},{16,12}... | collective-permute-start | bytes 393224 | tf_op jit(solution)/shard_map/ppermute | solution.py:25
  104.7 14.0 %collective-permute-start.14 = (f32[1,128,256]{2,1,0:T(8,128)S(1)}, f32[1,128,256]{2,1,0:T(8,128)S(1)}, u32[]{:S(2)}, u32[]{:S(2)}) collective-permute-start(f32[1,128,256]{2,1,0:T(8,128)S(1)} %copy-done.4), channel_id=1, source_target_pairs={{0,30},{2,28},{4,26},{6,24},{8,22},{10,20},{12,18},{14,16},{16,14}... | collective-permute-start | bytes 393224 | tf_op jit(solution)/shard_map/ppermute | solution.py:25
  117.4 119.8 %all-reduce.2.cloned.1.call-start = ((), (), s32[]{:S(2)}) async-start(), calls=%async_computation.5 | async-start | bytes 262144 | tf_op jit(solution)/shard_map/psum | solution.py:70
  119.4 2.3 copy-start.14
Sparse Core Ops, SparseCore 0:
  75.4 9.5 reduce-scatter.2
  117.5 7.6 reduce-scatter.4
  130.6 106.5 all-reduce.1
